TPU v7x, 32 devices: a whole 2x2x4 slice. The times are simulated.
32 devices in a mesh: grp: 2 (over x), space: 16 (over z, y, core).
Axes of the slice: x: 2, y: 2, z: 4, core: 2. Of those that a mesh axis runs over, the one named last changes fastest.
Arguments:
- propagator: bfloat16 [4, 3, 4, 12, 32768], P('grp', None, None, None, 'space'), parts along dimension 0, may hold values from -6 to 6
- eigvecs: bfloat16 [4, 3, 256, 32768], P('grp', None, None, 'space'), parts along dimension 0, may hold values from -6 to 6
- operator_weights: float32 [256, 2, 256], P('grp'), parts along dimension 0, may hold values from -0.375 to 0.375
- sink_time: int32 [2], P('grp'), parts along dimension 0, may hold values from 0 to 127
- term_index: int32 [48, 3], replicated, may hold values from 0 to 11
- term_sign: int32 [48], replicated, may hold values from 0 to 1
- solver_order: int32 [32768], P('space'), may hold values from 0 to 32767, as said below
Outputs:
- solver_source: bfloat16 [4, 3, 4, 12, 32768], P('grp', None, None, None, 'space'), parts along dimension 0
There are 2 independent parts, one for each index of `grp`. A program takes and returns all parts, laid end to end along the dimension named above; an argument that names none is the same for every part. Nothing has to cross between parts.
Inputs may be any that keep to these rules, and one draw needn't show every extreme that they name: solver_order is a permutation of the sites; split into blocks of 2048 positions and each block into pieces of 128, piece d of block e holds only sites d * 2048 to (d + 1) * 2048 - 1.
All inputs are finite; a program needn't handle non-finite values.
Results may differ from a plain program's by a relative error of at most 0.006.
Values may be sent and summed in bfloat16 or wider, within the bound.
A program may use at most 64 MiB of HBM per device.

v0:
```python
import math
import jax
import jax.numpy as jnp
from jax import lax
from jax.sharding import PartitionSpec as P

NVEC = 256
NMOM = 4
EXTENT = 64
MOMENTA = ((0, 0, 0), (1, 0, 0), (0, 1, 0), (0, 0, 1))
PRECISE = lax.Precision.HIGHEST


def phase_tables(offset, length):
    site_index = offset + jnp.arange(length, dtype=jnp.int32)
    coord_x = site_index % EXTENT
    coord_y = site_index // EXTENT % EXTENT
    coord_z = site_index // (EXTENT * EXTENT)
    windings = jnp.stack(
        [
            (step_x * coord_x + step_y * coord_y + step_z * coord_z) % EXTENT
            for step_x, step_y, step_z in MOMENTA
        ]
    )
    angles = windings.astype(jnp.float32) * (2.0 * math.pi / EXTENT)
    return (jnp.cos(angles), jnp.sin(angles))


def phased_rows(prop_colour, cosine_table, sine_table):
    real_part = prop_colour[0].astype(jnp.float32)[None]
    imag_part = prop_colour[1].astype(jnp.float32)[None]
    cos_rows = cosine_table[:, None, None, :]
    sin_rows = sine_table[:, None, None, :]
    turned = jnp.stack(
        [cos_rows * real_part + sin_rows * imag_part, cos_rows * imag_part - sin_rows * real_part]
    )
    return turned.astype(jnp.bfloat16).reshape(-1, turned.shape[-1])


def project(eig_colour, phased, scale_in):
    site_dims = (((1,), (1,)), ((), ()))
    from_real = lax.dot_general(
        eig_colour[0], phased, site_dims, preferred_element_type=jnp.float32
    ).reshape(-1, 2, NMOM, 48)
    from_imag = lax.dot_general(
        eig_colour[1], phased, site_dims, preferred_element_type=jnp.float32
    ).reshape(-1, 2, NMOM, 48)
    real_part = from_real[:, 0] + from_imag[:, 1]
    imag_part = from_real[:, 1] - from_imag[:, 0]
    return jnp.stack([real_part, imag_part]) * scale_in


def assemble(pieces):
    stacked = jnp.stack(pieces)
    vectors = stacked.shape[2]
    return stacked.transpose(3, 1, 2, 0, 4).reshape(NMOM, 2, vectors, 144)


def weighted_total(blocks, weights):
    real_sum = jnp.einsum("k,pkc->pc", weights[0], blocks[:, 0], precision=PRECISE) - jnp.einsum(
        "k,pkc->pc", weights[1], blocks[:, 1], precision=PRECISE
    )
    imag_sum = jnp.einsum("k,pkc->pc", weights[0], blocks[:, 1], precision=PRECISE) + jnp.einsum(
        "k,pkc->pc", weights[1], blocks[:, 0], precision=PRECISE
    )
    return jnp.stack([real_sum, imag_sum], axis=1)


def term_tables(term_index, term_sign):
    channels = jnp.arange(12, dtype=jnp.int32)
    first_pick = (term_index[:, 0:1] == channels[None]).astype(jnp.float32)
    second_pick = (term_index[:, 1:2] == channels[None]).astype(jnp.float32)
    sign_values = (2 * term_sign - 1).astype(jnp.float32)
    placement = (term_index[None, :, 2] == channels[:, None]).astype(jnp.float32) * sign_values[
        None
    ]
    return (first_pick, second_pick, placement)


def contract(blocks, weighted, first_pick, second_pick, placement):
    vectors = blocks.shape[2]
    block_grid = blocks.reshape(NMOM, 2, vectors, 12, 12)
    first_terms = jnp.einsum("mi,pqkij->pqkmj", first_pick, block_grid, precision=PRECISE)
    second_terms = jnp.einsum(
        "mi,pqij->pqmj", second_pick, weighted.reshape(NMOM, 2, 12, 12), precision=PRECISE
    )[:, :, None]
    real_part = first_terms[:, 0] * second_terms[:, 0] - first_terms[:, 1] * second_terms[:, 1]
    imag_part = first_terms[:, 0] * second_terms[:, 1] + first_terms[:, 1] * second_terms[:, 0]
    product = jnp.stack([real_part, imag_part], axis=1)
    return jnp.einsum("cm,pqkmj->pqkcj", placement, product, precision=PRECISE).reshape(
        NMOM, 2, vectors, 144
    )


def rebuild(coeffs, eig_colour, colour, cosine_table, sine_table, scale_out):
    vectors = coeffs.shape[2]
    colour_block = coeffs.reshape(NMOM, 2, vectors, 3, 48)[:, :, :, colour]
    coeff_table = colour_block.transpose(2, 1, 0, 3).reshape(vectors, 2 * NMOM * 48)
    vector_dims = (((0,), (0,)), ((), ()))
    from_real = lax.dot_general(
        coeff_table, eig_colour[0], vector_dims, preferred_element_type=jnp.float32
    ).reshape(2, NMOM, 48, -1)
    from_imag = lax.dot_general(
        coeff_table, eig_colour[1], vector_dims, preferred_element_type=jnp.float32
    ).reshape(2, NMOM, 48, -1)
    real_part = from_real[0] - from_imag[1]
    imag_part = from_real[1] + from_imag[0]
    cos_rows = cosine_table[:, None, :]
    sin_rows = sine_table[:, None, :]
    out_real = jnp.sum(cos_rows * real_part - sin_rows * imag_part, axis=0)
    out_imag = jnp.sum(cos_rows * imag_part + sin_rows * real_part, axis=0)
    return jnp.stack([out_real, out_imag]) * scale_out


def on_device(
    propagator, eigvecs, operator_weights, sink_time, term_index, term_sign, solver_order
):
    length = propagator.shape[-1]
    devices = lax.axis_size("space")
    offset = lax.axis_index("space") * length
    cosine_table, sine_table = phase_tables(offset, length)
    scale_in = 1.0 / math.sqrt(3.0 * length * devices)
    pieces = []
    for colour in range(3):
        phased = phased_rows(propagator[:, colour], cosine_table, sine_table)
        pieces.append(project(eigvecs[:, colour], phased, scale_in))
    partial_blocks = assemble(pieces)
    weights = lax.dynamic_index_in_dim(operator_weights, sink_time[0], 0, keepdims=False)
    first_pick, second_pick, placement = term_tables(term_index, term_sign)
    blocks = lax.psum(partial_blocks, "space")
    weighted = weighted_total(blocks, weights)
    coeffs = contract(blocks, weighted, first_pick, second_pick, placement).astype(jnp.bfloat16)
    scale_out = 1.0 / math.sqrt(NMOM * NVEC)
    colours = [
        rebuild(coeffs, eigvecs[:, colour], colour, cosine_table, sine_table, scale_out)
        for colour in range(3)
    ]
    source = jnp.stack(colours, axis=1).astype(jnp.bfloat16).reshape(2 * 3 * 48, length)
    wanted = lax.all_to_all(
        solver_order.reshape(devices, -1), "space", split_axis=0, concat_axis=0, tiled=True
    )
    local_index = wanted.reshape(length) - offset
    picked = jnp.take(source, local_index, axis=1)
    placed = lax.all_to_all(picked, "space", split_axis=1, concat_axis=1, tiled=True)
    return placed.reshape(2, 3, 4, 12, length)


def solution(mesh):
    return jax.shard_map(
        on_device,
        mesh=mesh,
        in_specs=(
            P("grp", None, None, None, "space"),
            P("grp", None, None, "space"),
            P("grp", None, None),
            P("grp"),
            P(),
            P(),
            P("space"),
        ),
        out_specs=P("grp", None, None, None, "space"),
        check_vma=False,
    )
```

profile of v0, /device:TPU:0, one launch (start us, length us, event | category | flops | bytes accessed | tf_op | source)
XLA Modules:
  0.0 206.0 jit_solution(521534441980782932)
XLA Ops:
  6.5 0.2 and_select_fusion
  6.7 0.1 and_select_fusion.5
  6.8 1.5 bitcast_convert_fusion.5
  8.3 0.2 copy.37
  8.6 0.2 copy.38
  8.8 0.2 copy.40
  9.0 0.2 copy.41
  9.3 0.2 copy.43
  9.5 0.2 copy.44
  9.8 0.3 fusion.77
  10.0 2.7 %add_convert_fusion.2 = (bf16[1,4,4,12,2048]{4,3,2,1,0:T(8,128)(2,1)S(1)}, bf16[1,4,4,12,2048]{4,3,2,1,0:T(8,128)(2,1)S(1)}, bf16[1,4,4,12,2048]{4,3,2,1,0:T(8,1...) fusion(f32[4,12,2048]{2,1,0:T(8,128)S(1)} %copy.38, ...), kind=kLoop, calls=%fused_computation.16 | loop fusion | flops 9437184 | bytes 7143424 | tf_op jit(solution)/shard_map/convert.13
  12.8 0.3 pad_maximum_fusion
  13.1 1.4 convert_element_type.148
  14.4 3.2 %fusion.33 = f32[384,256]{1,0:T(8,128)} fusion(bf16[384,2048]{1,0:T(8,128)(2,1)} %convert_element_type.148, bf16[2,3,256,2048]{3,2,1,0:T(8,128)(2,1)} %param.8), kind=kOutput, calls=%fused_computation.58 | convolution fusion | flops 402653184 | bytes 3014656 | tf_op jit(solution)/shard_map/dot_general | solution.py:42
  17.6 2.7 %fusion.29 = f32[384,256]{1,0:T(8,128)} fusion(bf16[384,2048]{1,0:T(8,128)(2,1)S(1)} %copy-done.6, bf16[2,3,256,2048]{3,2,1,0:T(8,128)(2,1)} %param.8), kind=kOutput, calls=%fused_computation.54 | convolution fusion | flops 402653184 | bytes 3014656 | tf_op jit(solution)/shard_map/dot_general | solution.py:45
  20.4 0.3 pad_maximum_fusion.1
  20.6 1.4 convert_element_type.153
  22.0 3.2 %fusion.25 = f32[384,256]{1,0:T(8,128)} fusion(bf16[384,2048]{1,0:T(8,128)(2,1)} %convert_element_type.153, bf16[2,3,256,2048]{3,2,1,0:T(8,128)(2,1)} %param.8), kind=kOutput, calls=%fused_computation.50 | convolution fusion | flops 402653184 | bytes 3014656 | tf_op jit(solution)/shard_map/dot_general | solution.py:42
  25.2 2.7 %fusion.21 = f32[384,256]{1,0:T(8,128)} fusion(bf16[384,2048]{1,0:T(8,128)(2,1)S(1)} %copy-done.7, bf16[2,3,256,2048]{3,2,1,0:T(8,128)(2,1)} %param.8), kind=kOutput, calls=%fused_computation.46 | convolution fusion | flops 402653184 | bytes 3014656 | tf_op jit(solution)/shard_map/dot_general | solution.py:45
  27.9 0.3 pad_maximum_fusion.2
  28.2 1.4 convert_element_type.158
  29.5 2.4 %fusion.17 = f32[384,256]{1,0:T(8,128)S(1)} fusion(bf16[384,2048]{1,0:T(8,128)(2,1)} %convert_element_type.158, bf16[2,3,256,2048]{3,2,1,0:T(8,128)(2,1)} %param.8), kind=kOutput, calls=%fused_computation.42 | convolution fusion | flops 402653184 | bytes 3014656 | tf_op jit(solution)/shard_map/dot_general | solution.py:42
  32.0 1.9 fusion.13
  33.9 0.1 fusion.59
  34.0 0.8 copy-done.9
  34.9 0.1 copy-done.10
  35.2 1.1 pad_maximum_fusion.3
  36.4 7.4 %all-to-all-start = ((s32[16,1,128]{2,1,0:T(1,128)}), s32[16,1,128]{2,1,0:T(1,128)S(1)}, u32[]{:S(2)}, u32[]{:S(2)}) async-start(s32[16,1,128]{2,1,0:T(1,128)} %bitcast), calls=%async_computation | async-start | bytes 16384 | tf_op jit(solution)/shard_map/all_to_all | solution.py:139
  44.5 5.7 %all-to-all-done = s32[16,1,128]{2,1,0:T(1,128)S(1)} async-done(((s32[16,1,128]{2,1,0:T(1,128)}), s32[16,1,128]{2,1,0:T(1,128)S(1)}, u32[]{:S(2)}, u32[]{:S(2)}) %all-to-all-start) | async-done | bytes 8224 | tf_op jit(solution)/shard_map/all_to_all | solution.py:139
  50.2 83.1 %all-reduce.2.cloned.1.call-done = f32[4,2,256,144]{2,3,1,0:T(8,128)} async-done(((f32[4,2,256,144]{2,3,1,0:T(8,128)}), f32[4,2,256,144]{2,3,1,0:T(8,128)}) %all-reduce.2.cloned.1.call-update) | async-done | bytes 1179664 | tf_op jit(solution)/shard_map/psum | solution.py:130
  133.4 1.7 fusion.51
  135.1 1.7 fusion.53
  136.8 0.1 stack.123
  136.9 0.1 copy.48
  137.0 0.6 fusion.50
  137.6 0.6 fusion.52
  138.2 0.1 stack.124
  138.3 0.1 copy.49
  138.4 0.2 convolution_bitcast_fusion.1
  138.6 0.9 copy.46
  139.5 2.1 %convolution_bitcast_fusion = f32[4,2,256,48,12]{2,3,4,1,0:T(8,128)S(1)} fusion(f32[4,2,256,12,12]{2,1,4,3,0:T(2,128)S(1)} %bitcast.204, s32[48]{0:T(128)S(1)} %get-tuple-element.55), kind=kOutput, calls=%fused_computation.7 | convolution fusion | flops 169869888 | bytes 5898432 | tf_op jit(solution)/shard_map/mi,pqkij->pqkmj/dot_general | solution.py:83
  141.7 0.9 multiply_subtract_fusion
  142.5 2.5 %fusion.8 = bf16[4,2,256,12,12]{2,3,4,1,0:T(8,128)(2,1)S(1)} fusion(f32[4,1,256,48,12]{2,3,4,1,0:T(8,128)S(1)} %get-tuple-element.24, f32[4,1,256,48,12]{2,3,4,1,0:T(8,128)S(1)} %get-tuple-element.23, f32[48]{0:T(128)S(1)} %add_convert_fusion.4, s32[48]{0:T(128)S(1)} %get-tuple-element.54), kind=kOutput, calls=%fused_computation.31 | convolution fusion | flops 171345024 | bytes 5308800 | tf_op jit(solution)/shard_map/cm,pqkmj->pqkcj/dot_general | solution.py:90
  145.1 0.6 copy.50
  145.7 0.5 fusion.86
  146.3 0.6 fusion.11
  146.8 0.6 fusion.15
  147.5 0.6 fusion.19
  148.0 0.6 fusion.23
  148.7 0.6 fusion.27
  149.2 0.6 fusion.31
  149.8 0.6 slice_add_fusion
  150.5 0.7 slice_add_fusion.1
  151.2 0.7 slice_subtract_fusion.2
  151.8 1.4 subtract_reduce_fusion.2
  153.4 0.1 pad_maximum_fusion.4
  153.6 0.8 copy.57
  154.4 7.5 %gather_fusion = bf16[2048,288]{1,0:T(8,128)(2,1)S(1)} fusion(bf16[288,2048]{0,1:T(8,128)(2,1)S(1)} %copy.57, s32[2048]{0:T(1024)S(1)} %broadcast_clamp_fusion), kind=kCustom, calls=%fused_computation | custom fusion | bytes 2367488 | tf_op jit(solution)/shard_map/jit(_take)/gather | solution.py:143
  161.9 0.9 copy.58
  162.8 0.1 broadcast_select_fusion
  162.9 33.0 %all_to_all.15 = bf16[288,16,128]{2,0,1:T(8,128)(2,1)S(1)} all-to-all(bf16[288,16,128]{2,0,1:T(8,128)(2,1)S(1)} %broadcast_select_fusion), channel_id=1, replica_groups=mesh['grp'=2,'space'=16] {'space'}, dimensions={1} | all-to-all | bytes 2359296 | tf_op jit(solution)/shard_map/all_to_all | solution.py:144
  195.9 0.5 copy.59
  196.4 0.8 reshape.956
  197.2 1.9 copy.60
  (55 shorter events, 0.6 us)
Async XLA Ops:
  6.5 126.8 %copy-start = (f32[128,2,256]{2,1,0:T(2,128)S(1)}, f32[128,2,256]{2,1,0:T(2,128)}, u32[]{:S(2)}) copy-start(f32[128,2,256]{2,1,0:T(2,128)} %param.9) | copy-start | bytes 786436
  6.5 126.8 %all-reduce.2.cloned.1.call-start = ((), (), s32[]{:S(2)}) async-start(), calls=%async_computation.2 | async-start | bytes 2359296 | tf_op jit(solution)/shard_map/psum | solution.py:130
  14.4 3.2 %copy-start.6 = (bf16[384,2048]{1,0:T(8,128)(2,1)S(1)}, bf16[384,2048]{1,0:T(8,128)(2,1)}, u32[]{:S(2)}) copy-start(bf16[384,2048]{1,0:T(8,128)(2,1)} %convert_element_type.148) | copy-start | bytes 4718596
  17.6 2.7 %copy-start.4 = (bf16[1,4,4,12,2048]{4,3,2,1,0:T(8,128)(2,1)S(1)}, bf16[1,4,4,12,2048]{4,3,2,1,0:T(8,128)(2,1)}, u32[]{:S(2)}) copy-start(bf16[1,4,4,12,2048]{4,3,2,1,0:T(8,128)(2,1)} %get-tuple-element.48) | copy-start | bytes 2359300
  17.6 2.7 %copy-start.5 = (bf16[1,4,4,12,2048]{4,3,2,1,0:T(8,128)(2,1)S(1)}, bf16[1,4,4,12,2048]{4,3,2,1,0:T(8,128)(2,1)}, u32[]{:S(2)}) copy-start(bf16[1,4,4,12,2048]{4,3,2,1,0:T(8,128)(2,1)} %get-tuple-element.49) | copy-start | bytes 2359300
  22.0 3.2 %copy-start.7 = (bf16[384,2048]{1,0:T(8,128)(2,1)S(1)}, bf16[384,2048]{1,0:T(8,128)(2,1)}, u32[]{:S(2)}) copy-start(bf16[384,2048]{1,0:T(8,128)(2,1)} %convert_element_type.153) | copy-start | bytes 4718596
  25.2 2.7 %copy-start.3 = (bf16[1,4,4,12,2048]{4,3,2,1,0:T(8,128)(2,1)S(1)}, bf16[1,4,4,12,2048]{4,3,2,1,0:T(8,128)(2,1)}, u32[]{:S(2)}) copy-start(bf16[1,4,4,12,2048]{4,3,2,1,0:T(8,128)(2,1)} %get-tuple-element.51) | copy-start | bytes 2359300
  29.5 2.4 %copy-start.8 = (bf16[384,2048]{1,0:T(8,128)(2,1)S(1)}, bf16[384,2048]{1,0:T(8,128)(2,1)}, u32[]{:S(2)}) copy-start(bf16[384,2048]{1,0:T(8,128)(2,1)} %convert_element_type.158) | copy-start | bytes 4718596
  32.0 2.0 copy-start.11
  32.0 2.0 copy-start.12
  33.9 1.0 copy-start.9
  33.9 1.1 copy-start.10
  35.2 8.6 %copy-start.13 = (s32[48,3]{0,1:T(4,128)S(1)}, s32[48,3]{0,1:T(4,128)}, u32[]{:S(2)}) copy-start(s32[48,3]{0,1:T(4,128)} %param.11) | copy-start | bytes 1732
  35.2 8.6 %copy-start.14 = (s32[48]{0:T(128)S(1)}, s32[48]{0:T(128)}, u32[]{:S(2)}) copy-start(s32[48]{0:T(128)} %param.12) | copy-start | bytes 580
  36.4 13.8 %all-to-all-start = ((s32[16,1,128]{2,1,0:T(1,128)}), s32[16,1,128]{2,1,0:T(1,128)S(1)}, u32[]{:S(2)}, u32[]{:S(2)}) async-start(s32[16,1,128]{2,1,0:T(1,128)} %bitcast), calls=%async_computation | async-start | bytes 16384 | tf_op jit(solution)/shard_map/all_to_all | solution.py:139
  133.4 3.6 %copy-start.2 = (f32[4,2,256,144]{2,3,1,0:T(8,128)S(1)}, f32[4,2,256,144]{2,3,1,0:T(8,128)}, u32[]{:S(2)}) copy-start(f32[4,2,256,144]{2,3,1,0:T(8,128)} %all-reduce.2.cloned.1.call-done) | copy-start | bytes 3538948
  139.5 6.7 %slice-start = ((s8[6291456]{0:T(1024)(128)(4,1)}), s8[4194304]{0:T(1024)(128)(4,1)S(1)}, s32[]{:S(2)}) async-start(s8[6291456]{0:T(1024)(128)(4,1)} %bitcast.211), calls=%async_computation.3 | async-start | bytes 8388608
  141.7 4.6 %slice-start.1 = ((s8[6291456]{0:T(1024)(128)(4,1)}), s8[2097152]{0:T(1024)(128)(4,1)S(1)}, s32[]{:S(2)}) async-start(s8[6291456]{0:T(1024)(128)(4,1)} %bitcast.211), calls=%async_computation.4 | async-start | bytes 4194304
  196.4 2.8 %copy-start.1 = (f32[128,2,256]{2,1,0:T(2,128)S(1)}, f32[128,2,256]{2,1,0:T(2,128)}, u32[]{:S(2)}) copy-start(f32[128,2,256]{2,1,0:T(2,128)} %param.9) | copy-start | bytes 786436
Sparse Core Ops, SparseCore 0:
  36.5 96.7 all-reduce.1
where the time goes:
time: 206 us
  waiting for transfers between devices  88.8 us (43%)
  blocking collectives  33 us (16%)
  matrix products  29 us (14%)
  local copies, waits for them, and re-layouts  21.5 us (10%)
  between operations  14.6 us (7%)
  other arithmetic  11.7 us (6%)
  starting transfers between devices  7.44 us (4%)
    psum x1, waiting for transfers between devices, on_device(): blocks = lax.psum(partial_blocks, 'space')  83.1 us
    all_to_all x1, blocking collectives, on_device(): lax.all_to_all(picked, 'space', split_axis=1, concat_axis=1, tiled=True)  33 us
    dot_general x3, matrix products, project(): lax.dot_general(eig_colour[0], phased, site_dims, preferred_element_type=...  8.78 us
    gather x2, local copies, waits for them, and re-layouts, on_device(): picked = jnp.take(source, local_index, axis=1)  8.36 us
    all_to_all x1, starting transfers between devices, on_device(): lax.all_to_all(solver_order.reshape(devices, -1), 'space', split_axis=0,...  7.43 us
    dot_general x3, matrix products, project(): lax.dot_general(eig_colour[1], phased, site_dims, preferred_element_type=...  7.31 us
    all_to_all x1, waiting for transfers between devices, on_device(): lax.all_to_all(solver_order.reshape(devices, -1), 'space', split_axis=0,...  5.65 us
    convert_element_type x3, local copies, waits for them, and re-layouts, phased_rows(): return turned.astype(jnp.bfloat16).reshape(-1, turned.shape[-1])  4.12 us
  transfers between devices with their start and end apart: 2, of which 2 were waited for; matrix products, arithmetic and copies ran while one was open for 0% of the time, Pallas kernels for 0%

commit v1 on v0

--- a/solution.py
+++ b/solution.py
@@ -9,6 +9,18 @@
 EXTENT = 64
 MOMENTA = ((0, 0, 0), (1, 0, 0), (0, 1, 0), (0, 0, 1))
 PRECISE = lax.Precision.HIGHEST
+
+
+def cut_along(value, dim, size):
+    shape = value.shape
+    tiles = value.reshape(*shape[:dim], size, shape[dim] // size, *shape[dim + 1 :])
+    return jnp.moveaxis(tiles, dim, 0)
+
+
+def joined_along(tiles, dim):
+    dims = list(tiles.shape[1:])
+    dims[dim] *= tiles.shape[0]
+    return jnp.moveaxis(tiles, 0, dim).reshape(dims)
 
 
 def phase_tables(offset, length):
@@ -136,9 +148,15 @@
         for colour in range(3)
     ]
     source = jnp.stack(colours, axis=1).astype(jnp.bfloat16).reshape(2 * 3 * 48, length)
-    wanted = lax.all_to_all(
-        solver_order.reshape(devices, -1), "space", split_axis=0, concat_axis=0, tiled=True
-    )
+    x = solver_order.reshape(devices, -1)
+    size, index = (lax.axis_size("space"), lax.axis_index("space"))
+    tiles = cut_along(x, 0, size)
+    gathered = [tiles[index]]
+    for step in range(1, size):
+        sent = tiles[index ^ step]
+        gathered.append(lax.ppermute(sent, "space", [(i, i ^ step) for i in range(size)]))
+    tiles = jnp.stack(gathered)[index ^ jnp.arange(size)]
+    wanted = joined_along(tiles, 0)
     local_index = wanted.reshape(length) - offset
     picked = jnp.take(source, local_index, axis=1)
     placed = lax.all_to_all(picked, "space", split_axis=1, concat_axis=1, tiled=True)

time: 206 us -> 207 us (level)
  waiting for transfers between devices: 88.8 us -> 73.1 us
  starting transfers between devices: 7.44 us -> 22.4 us
    ppermute x0 -> x15, starting transfers between devices: none -> 22.4 us  [on_device(): lax.ppermute(sent, 'space', [(i, i ^ step) for i in range(size)])]
    psum x1, waiting for transfers between devices: 83.1 us -> 69.1 us  [on_device(): blocks = lax.psum(partial_blocks, 'space')]
    all_to_all x1 -> x0, starting transfers between devices: 7.43 us -> none  [on_device(): lax.all_to_all(solver_order.reshape(devices, -1), 'space', split_axis=0,...]
    all_to_all x1 -> x0, waiting for transfers between devices: 5.65 us -> none  [on_device(): lax.all_to_all(solver_order.reshape(devices, -1), 'space', split_axis=0,...]
    ppermute x0 -> x15, waiting for transfers between devices: none -> 3.96 us  [on_device(): lax.ppermute(sent, 'space', [(i, i ^ step) for i in range(size)])]
  transfers between devices with their start and end apart: 2 -> 16, of which waited for: 2 -> 3; matrix products, arithmetic and copies ran while one was open for 0% -> 0% of each run, Pallas kernels for 0% -> 0%
where the time goes in v1:
time: 207 us; the launch traced here: 206 us
  waiting for transfers between devices  73.1 us (35%)
  blocking collectives  33 us (16%)
  matrix products  28.9 us (14%)
  starting transfers between devices  22.4 us (11%)
  local copies, waits for them, and re-layouts  22.2 us (11%)
  between operations  14.8 us (7%)
  other arithmetic  11.9 us (6%)
    psum x1, waiting for transfers between devices, on_device(): blocks = lax.psum(partial_blocks, 'space')  69.1 us
    all_to_all x1, blocking collectives, on_device(): lax.all_to_all(picked, 'space', split_axis=1, concat_axis=1, tiled=True)  33 us
    ppermute x15, starting transfers between devices, on_device(): lax.ppermute(sent, 'space', [(i, i ^ step) for i in range(size)])  22.4 us
    dot_general x3, matrix products, project(): lax.dot_general(eig_colour[0], phased, site_dims, preferred_element_type=...  8.74 us
    gather x2, local copies, waits for them, and re-layouts, on_device(): picked = jnp.take(source, local_index, axis=1)  8.36 us
    dot_general x3, matrix products, project(): lax.dot_general(eig_colour[1], phased, site_dims, preferred_element_type=...  7.3 us
  transfers between devices with their start and end apart: 16, of which 3 were waited for; matrix products, arithmetic and copies ran while one was open for 0% of the time, Pallas kernels for 0%

profile of v1, /device:TPU:0, one launch (start us, length us, event | category | flops | bytes accessed | tf_op | source)
XLA Modules:
  0.0 206.3 jit_solution(3720682918315767384)
XLA Ops:
  6.8 1.5 bitcast_convert_fusion.5
  8.3 0.2 copy.82
  8.6 0.2 copy.83
  8.8 0.2 copy.85
  9.0 0.2 copy.86
  9.3 0.2 copy.88
  9.5 0.2 copy.89
  9.8 0.3 fusion.77
  10.0 2.8 %add_convert_fusion.2 = (bf16[1,4,4,12,2048]{4,3,2,1,0:T(8,128)(2,1)S(1)}, bf16[1,4,4,12,2048]{4,3,2,1,0:T(8,128)(2,1)S(1)}, bf16[1,4,4,12,2048]{4,3,2,1,0:T(8,1...) fusion(f32[4,12,2048]{2,1,0:T(8,128)S(1)} %copy.83, ...), kind=kLoop, calls=%fused_computation.17 | loop fusion | flops 9437184 | bytes 7143424 | tf_op jit(solution)/shard_map/convert.13
  12.8 0.3 pad_maximum_fusion
  13.1 1.4 convert_element_type.148
  14.4 3.2 %fusion.33 = f32[384,256]{1,0:T(8,128)} fusion(bf16[384,2048]{1,0:T(8,128)(2,1)} %convert_element_type.148, bf16[2,3,256,2048]{3,2,1,0:T(8,128)(2,1)} %param.8), kind=kOutput, calls=%fused_computation.59 | convolution fusion | flops 402653184 | bytes 3014656 | tf_op jit(solution)/shard_map/dot_general | solution.py:54
  17.6 2.7 %fusion.29 = f32[384,256]{1,0:T(8,128)} fusion(bf16[384,2048]{1,0:T(8,128)(2,1)S(1)} %copy-done.6, bf16[2,3,256,2048]{3,2,1,0:T(8,128)(2,1)} %param.8), kind=kOutput, calls=%fused_computation.55 | convolution fusion | flops 402653184 | bytes 3014656 | tf_op jit(solution)/shard_map/dot_general | solution.py:57
  20.4 0.3 pad_maximum_fusion.1
  20.6 1.4 convert_element_type.153
  22.0 3.2 %fusion.25 = f32[384,256]{1,0:T(8,128)} fusion(bf16[384,2048]{1,0:T(8,128)(2,1)} %convert_element_type.153, bf16[2,3,256,2048]{3,2,1,0:T(8,128)(2,1)} %param.8), kind=kOutput, calls=%fused_computation.51 | convolution fusion | flops 402653184 | bytes 3014656 | tf_op jit(solution)/shard_map/dot_general | solution.py:54
  25.2 2.7 %fusion.21 = f32[384,256]{1,0:T(8,128)} fusion(bf16[384,2048]{1,0:T(8,128)(2,1)S(1)} %copy-done.7, bf16[2,3,256,2048]{3,2,1,0:T(8,128)(2,1)} %param.8), kind=kOutput, calls=%fused_computation.47 | convolution fusion | flops 402653184 | bytes 3014656 | tf_op jit(solution)/shard_map/dot_general | solution.py:57
  27.8 0.3 pad_maximum_fusion.2
  28.1 1.4 convert_element_type.158
  29.5 2.4 %fusion.17 = f32[384,256]{1,0:T(8,128)S(1)} fusion(bf16[384,2048]{1,0:T(8,128)(2,1)} %convert_element_type.158, bf16[2,3,256,2048]{3,2,1,0:T(8,128)(2,1)} %param.8), kind=kOutput, calls=%fused_computation.43 | convolution fusion | flops 402653184 | bytes 3014656 | tf_op jit(solution)/shard_map/dot_general | solution.py:54
  32.0 1.9 fusion.13
  34.0 0.8 copy-done.9
  35.2 1.1 pad_maximum_fusion.3
  36.6 3.1 %collective-permute-start.3 = (s32[1,128]{1,0:T(1,128)S(1)}, s32[1,128]{1,0:T(1,128)S(1)}, u32[]{:S(2)}, u32[]{:S(2)}) collective-permute-start(s32[1,128]{1,0:T(1,128)S(1)} %get-tuple-element.65), channel_id=1, source_target_pairs={{0,4},{1,5},{2,6},{3,7},{4,0},{5,1},{6,2},{7,3},{8,12},{9,13},{10,... | collective-permute-start | bytes 1544 | tf_op jit(solution)/shard_map/ppermute | solution.py:157
  39.7 2.1 %collective-permute-start.5 = (s32[1,128]{1,0:T(1,128)S(1)}, s32[1,128]{1,0:T(1,128)S(1)}, u32[]{:S(2)}, u32[]{:S(2)}) collective-permute-start(s32[1,128]{1,0:T(1,128)S(1)} %get-tuple-element.63), channel_id=1, source_target_pairs={{0,6},{1,7},{2,4},{3,5},{4,2},{5,3},{6,0},{7,1},{8,14},{9,15},{10,... | collective-permute-start | bytes 1544 | tf_op jit(solution)/shard_map/ppermute | solution.py:157
  41.8 0.6 collective-permute-start.6
  42.4 2.7 %collective-permute-start.7 = (s32[1,128]{1,0:T(1,128)S(1)}, s32[1,128]{1,0:T(1,128)S(1)}, u32[]{:S(2)}, u32[]{:S(2)}) collective-permute-start(s32[1,128]{1,0:T(1,128)S(1)} %get-tuple-element.61), channel_id=1, source_target_pairs={{0,8},{1,9},{2,10},{3,11},{4,12},{5,13},{6,14},{7,15},{8,0},{9,1},... | collective-permute-start | bytes 1544 | tf_op jit(solution)/shard_map/ppermute | solution.py:157
  45.9 0.3 collective-permute-start
  46.2 3.7 %collective-permute-start.9 = (s32[1,128]{1,0:T(1,128)S(1)}, s32[1,128]{1,0:T(1,128)S(1)}, u32[]{:S(2)}, u32[]{:S(2)}) collective-permute-start(s32[1,128]{1,0:T(1,128)S(1)} %get-tuple-element.59), channel_id=1, source_target_pairs={{0,10},{1,11},{2,8},{3,9},{4,14},{5,15},{6,12},{7,13},{8,2},{9,3},... | collective-permute-start | bytes 1544 | tf_op jit(solution)/shard_map/ppermute | solution.py:157
  49.9 3.3 %collective-permute-start.11 = (s32[1,128]{1,0:T(1,128)S(1)}, s32[1,128]{1,0:T(1,128)S(1)}, u32[]{:S(2)}, u32[]{:S(2)}) collective-permute-start(s32[1,128]{1,0:T(1,128)S(1)} %get-tuple-element.57), channel_id=1, source_target_pairs={{0,12},{1,13},{2,14},{3,15},{4,8},{5,9},{6,10},{7,11},{8,4},{9,5},... | collective-permute-start | bytes 1544 | tf_op jit(solution)/shard_map/ppermute | solution.py:157
  53.1 0.4 collective-permute-start.12
  53.5 4.4 %collective-permute-start.13 = (s32[1,128]{1,0:T(1,128)S(1)}, s32[1,128]{1,0:T(1,128)S(1)}, u32[]{:S(2)}, u32[]{:S(2)}) collective-permute-start(s32[1,128]{1,0:T(1,128)S(1)} %get-tuple-element.55), channel_id=1, source_target_pairs={{0,14},{1,15},{2,12},{3,13},{4,10},{5,11},{6,8},{7,9},{8,6},{9,7},... | collective-permute-start | bytes 1544 | tf_op jit(solution)/shard_map/ppermute | solution.py:157
  58.0 1.2 collective-permute-start.1
  59.2 0.5 collective-permute-start.2
  59.8 3.9 %collective-permute-done.14 = s32[1,128]{1,0:T(1,128)S(1)} collective-permute-done((s32[1,128]{1,0:T(1,128)S(1)}, s32[1,128]{1,0:T(1,128)S(1)}, u32[]{:S(2)}, u32[]{:S(2)}) %collective-permute-start.14) | collective-permute-done | bytes 544 | tf_op jit(solution)/shard_map/ppermute | solution.py:157
  63.7 0.6 gather_fusion
  64.3 69.1 %all-reduce.2.cloned.1.call-done = f32[4,2,256,144]{2,3,1,0:T(8,128)} async-done(((f32[4,2,256,144]{2,3,1,0:T(8,128)}), f32[4,2,256,144]{2,3,1,0:T(8,128)}) %all-reduce.2.cloned.1.call-update) | async-done | bytes 1179664 | tf_op jit(solution)/shard_map/psum | solution.py:142
  133.5 1.7 fusion.51
  135.2 1.7 fusion.53
  137.1 0.6 fusion.50
  137.7 0.6 fusion.52
  138.7 0.9 copy.91
  139.6 2.1 %convolution_bitcast_fusion = f32[4,2,256,48,12]{2,3,4,1,0:T(8,128)S(1)} fusion(f32[4,2,256,12,12]{2,1,4,3,0:T(2,128)S(1)} %bitcast.280, s32[48]{0:T(128)S(1)} %get-tuple-element.71), kind=kOutput, calls=%fused_computation.8 | convolution fusion | flops 169869888 | bytes 5898432 | tf_op jit(solution)/shard_map/mi,pqkij->pqkmj/dot_general | solution.py:95
  141.8 1.1 multiply_subtract_fusion
  142.9 2.5 %fusion.8 = bf16[4,2,256,12,12]{2,3,4,1,0:T(8,128)(2,1)S(1)} fusion(f32[4,1,256,48,12]{2,3,4,1,0:T(8,128)S(1)} %get-tuple-element.24, f32[4,1,256,48,12]{2,3,4,1,0:T(8,128)S(1)} %get-tuple-element.23, f32[48]{0:T(128)S(1)} %add_convert_fusion.4, s32[48]{0:T(128)S(1)} %get-tuple-element.70), kind=kOutput, calls=%fused_computation.32 | convolution fusion | flops 171345024 | bytes 5308800 | tf_op jit(solution)/shard_map/cm,pqkmj->pqkcj/dot_general | solution.py:102
  145.4 0.6 copy.95
  146.0 0.5 fusion.108
  146.6 0.6 fusion.11
  147.2 0.6 fusion.15
  147.8 0.6 fusion.19
  148.4 0.6 fusion.23
  149.0 0.6 fusion.27
  149.6 0.6 fusion.31
  150.2 0.6 slice_add_fusion
  150.8 0.7 slice_add_fusion.1
  151.5 0.7 slice_subtract_fusion.2
  152.2 1.4 subtract_reduce_fusion.2
  153.9 0.8 copy.102
  154.8 7.5 %gather_fusion.1 = bf16[2048,288]{1,0:T(8,128)(2,1)S(1)} fusion(bf16[288,2048]{0,1:T(8,128)(2,1)S(1)} %copy.102, s32[2048]{0:T(1024)S(1)} %broadcast_clamp_fusion), kind=kCustom, calls=%fused_computation.1 | custom fusion | bytes 2367488 | tf_op jit(solution)/shard_map/jit(_take)/gather | solution.py:161
  162.2 0.9 copy.103
  163.3 33.0 %all_to_all.6 = bf16[288,16,128]{2,0,1:T(8,128)(2,1)S(1)} all-to-all(bf16[288,16,128]{2,0,1:T(8,128)(2,1)S(1)} %broadcast_select_fusion), channel_id=1, replica_groups=mesh['grp'=2,'space'=16] {'space'}, dimensions={1} | all-to-all | bytes 2359296 | tf_op jit(solution)/shard_map/all_to_all | solution.py:162
  196.3 0.5 copy.104
  196.7 0.8 reshape.965
  197.6 1.9 copy.105
  (90 shorter events, 2.1 us)
Async XLA Ops:
  6.5 126.9 %copy-start = (f32[128,2,256]{2,1,0:T(2,128)S(1)}, f32[128,2,256]{2,1,0:T(2,128)}, u32[]{:S(2)}) copy-start(f32[128,2,256]{2,1,0:T(2,128)} %param.9) | copy-start | bytes 786436
  6.5 126.9 %all-reduce.2.cloned.1.call-start = ((), (), s32[]{:S(2)}) async-start(), calls=%async_computation.1 | async-start | bytes 2359296 | tf_op jit(solution)/shard_map/psum | solution.py:142
  14.4 3.2 %copy-start.6 = (bf16[384,2048]{1,0:T(8,128)(2,1)S(1)}, bf16[384,2048]{1,0:T(8,128)(2,1)}, u32[]{:S(2)}) copy-start(bf16[384,2048]{1,0:T(8,128)(2,1)} %convert_element_type.148) | copy-start | bytes 4718596
  17.6 2.7 %copy-start.4 = (bf16[1,4,4,12,2048]{4,3,2,1,0:T(8,128)(2,1)S(1)}, bf16[1,4,4,12,2048]{4,3,2,1,0:T(8,128)(2,1)}, u32[]{:S(2)}) copy-start(bf16[1,4,4,12,2048]{4,3,2,1,0:T(8,128)(2,1)} %get-tuple-element.48) | copy-start | bytes 2359300
  17.6 2.7 %copy-start.5 = (bf16[1,4,4,12,2048]{4,3,2,1,0:T(8,128)(2,1)S(1)}, bf16[1,4,4,12,2048]{4,3,2,1,0:T(8,128)(2,1)}, u32[]{:S(2)}) copy-start(bf16[1,4,4,12,2048]{4,3,2,1,0:T(8,128)(2,1)} %get-tuple-element.49) | copy-start | bytes 2359300
  22.0 3.2 %copy-start.7 = (bf16[384,2048]{1,0:T(8,128)(2,1)S(1)}, bf16[384,2048]{1,0:T(8,128)(2,1)}, u32[]{:S(2)}) copy-start(bf16[384,2048]{1,0:T(8,128)(2,1)} %convert_element_type.153) | copy-start | bytes 4718596
  25.2 2.7 %copy-start.3 = (bf16[1,4,4,12,2048]{4,3,2,1,0:T(8,128)(2,1)S(1)}, bf16[1,4,4,12,2048]{4,3,2,1,0:T(8,128)(2,1)}, u32[]{:S(2)}) copy-start(bf16[1,4,4,12,2048]{4,3,2,1,0:T(8,128)(2,1)} %get-tuple-element.51) | copy-start | bytes 2359300
  29.5 2.4 %copy-start.8 = (bf16[384,2048]{1,0:T(8,128)(2,1)S(1)}, bf16[384,2048]{1,0:T(8,128)(2,1)}, u32[]{:S(2)}) copy-start(bf16[384,2048]{1,0:T(8,128)(2,1)} %convert_element_type.158) | copy-start | bytes 4718596
  31.9 2.0 copy-start.11
  32.0 2.0 copy-start.12
  33.9 1.0 copy-start.9
  33.9 1.1 copy-start.10
  35.2 1.3 copy-start.13
  35.2 9.9 %copy-start.14 = (s32[48,3]{0,1:T(4,128)S(1)}, s32[48,3]{0,1:T(4,128)}, u32[]{:S(2)}) copy-start(s32[48,3]{0,1:T(4,128)} %param.11) | copy-start | bytes 1732
  35.2 9.9 %copy-start.15 = (s32[48]{0:T(128)S(1)}, s32[48]{0:T(128)}, u32[]{:S(2)}) copy-start(s32[48]{0:T(128)} %param.12) | copy-start | bytes 580
  36.6 9.2 %collective-permute-start.3 = (s32[1,128]{1,0:T(1,128)S(1)}, s32[1,128]{1,0:T(1,128)S(1)}, u32[]{:S(2)}, u32[]{:S(2)}) collective-permute-start(s32[1,128]{1,0:T(1,128)S(1)} %get-tuple-element.65), channel_id=1, source_target_pairs={{0,4},{1,5},{2,6},{3,7},{4,0},{5,1},{6,2},{7,3},{8,12},{9,13},{10,... | collective-permute-start | bytes 1544 | tf_op jit(solution)/shard_map/ppermute | solution.py:157
  39.7 6.2 %collective-permute-start.4 = (s32[1,128]{1,0:T(1,128)S(1)}, s32[1,128]{1,0:T(1,128)S(1)}, u32[]{:S(2)}, u32[]{:S(2)}) collective-permute-start(s32[1,128]{1,0:T(1,128)S(1)} %get-tuple-element.64), channel_id=1, source_target_pairs={{0,5},{1,4},{2,7},{3,6},{4,1},{5,0},{6,3},{7,2},{8,13},{9,12},{10,... | collective-permute-start | bytes 1544 | tf_op jit(solution)/shard_map/ppermute | solution.py:157
  39.7 6.5 %collective-permute-start.5 = (s32[1,128]{1,0:T(1,128)S(1)}, s32[1,128]{1,0:T(1,128)S(1)}, u32[]{:S(2)}, u32[]{:S(2)}) collective-permute-start(s32[1,128]{1,0:T(1,128)S(1)} %get-tuple-element.63), channel_id=1, source_target_pairs={{0,6},{1,7},{2,4},{3,5},{4,2},{5,3},{6,0},{7,1},{8,14},{9,15},{10,... | collective-permute-start | bytes 1544 | tf_op jit(solution)/shard_map/ppermute | solution.py:157
  41.8 8.0 %collective-permute-start.6 = (s32[1,128]{1,0:T(1,128)S(1)}, s32[1,128]{1,0:T(1,128)S(1)}, u32[]{:S(2)}, u32[]{:S(2)}) collective-permute-start(s32[1,128]{1,0:T(1,128)S(1)} %get-tuple-element.62), channel_id=1, source_target_pairs={{0,7},{1,6},{2,5},{3,4},{4,3},{5,2},{6,1},{7,0},{8,15},{9,14},{10,... | collective-permute-start | bytes 1544 | tf_op jit(solution)/shard_map/ppermute | solution.py:157
  42.4 7.5 %collective-permute-start.7 = (s32[1,128]{1,0:T(1,128)S(1)}, s32[1,128]{1,0:T(1,128)S(1)}, u32[]{:S(2)}, u32[]{:S(2)}) collective-permute-start(s32[1,128]{1,0:T(1,128)S(1)} %get-tuple-element.61), channel_id=1, source_target_pairs={{0,8},{1,9},{2,10},{3,11},{4,12},{5,13},{6,14},{7,15},{8,0},{9,1},... | collective-permute-start | bytes 1544 | tf_op jit(solution)/shard_map/ppermute | solution.py:157
  45.8 7.3 %collective-permute-start.8 = (s32[1,128]{1,0:T(1,128)S(1)}, s32[1,128]{1,0:T(1,128)S(1)}, u32[]{:S(2)}, u32[]{:S(2)}) collective-permute-start(s32[1,128]{1,0:T(1,128)S(1)} %get-tuple-element.60), channel_id=1, source_target_pairs={{0,9},{1,8},{2,11},{3,10},{4,13},{5,12},{6,15},{7,14},{8,1},{9,0},... | collective-permute-start | bytes 1544 | tf_op jit(solution)/shard_map/ppermute | solution.py:157
  45.9 7.7 %collective-permute-start = (s32[1,128]{1,0:T(1,128)S(1)}, s32[1,128]{1,0:T(1,128)S(1)}, u32[]{:S(2)}, u32[]{:S(2)}) collective-permute-start(s32[1,128]{1,0:T(1,128)S(1)} %get-tuple-element.68), channel_id=1, source_target_pairs={{0,1},{1,0},{2,3},{3,2},{4,5},{5,4},{6,7},{7,6},{8,9},{9,8},{10,11... | collective-permute-start | bytes 1544 | tf_op jit(solution)/shard_map/ppermute | solution.py:157
  46.2 11.8 %collective-permute-start.9 = (s32[1,128]{1,0:T(1,128)S(1)}, s32[1,128]{1,0:T(1,128)S(1)}, u32[]{:S(2)}, u32[]{:S(2)}) collective-permute-start(s32[1,128]{1,0:T(1,128)S(1)} %get-tuple-element.59), channel_id=1, source_target_pairs={{0,10},{1,11},{2,8},{3,9},{4,14},{5,15},{6,12},{7,13},{8,2},{9,3},... | collective-permute-start | bytes 1544 | tf_op jit(solution)/shard_map/ppermute | solution.py:157
  49.9 8.1 %collective-permute-start.10 = (s32[1,128]{1,0:T(1,128)S(1)}, s32[1,128]{1,0:T(1,128)S(1)}, u32[]{:S(2)}, u32[]{:S(2)}) collective-permute-start(s32[1,128]{1,0:T(1,128)S(1)} %get-tuple-element.58), channel_id=1, source_target_pairs={{0,11},{1,10},{2,9},{3,8},{4,15},{5,14},{6,13},{7,12},{8,3},{9,2},... | collective-permute-start | bytes 1544 | tf_op jit(solution)/shard_map/ppermute | solution.py:157
  49.9 9.4 %collective-permute-start.11 = (s32[1,128]{1,0:T(1,128)S(1)}, s32[1,128]{1,0:T(1,128)S(1)}, u32[]{:S(2)}, u32[]{:S(2)}) collective-permute-start(s32[1,128]{1,0:T(1,128)S(1)} %get-tuple-element.57), channel_id=1, source_target_pairs={{0,12},{1,13},{2,14},{3,15},{4,8},{5,9},{6,10},{7,11},{8,4},{9,5},... | collective-permute-start | bytes 1544 | tf_op jit(solution)/shard_map/ppermute | solution.py:157
  53.1 6.6 %collective-permute-start.12 = (s32[1,128]{1,0:T(1,128)S(1)}, s32[1,128]{1,0:T(1,128)S(1)}, u32[]{:S(2)}, u32[]{:S(2)}) collective-permute-start(s32[1,128]{1,0:T(1,128)S(1)} %get-tuple-element.56), channel_id=1, source_target_pairs={{0,13},{1,12},{2,15},{3,14},{4,9},{5,8},{6,11},{7,10},{8,5},{9,4},... | collective-permute-start | bytes 1544 | tf_op jit(solution)/shard_map/ppermute | solution.py:157
  53.5 6.3 %collective-permute-start.13 = (s32[1,128]{1,0:T(1,128)S(1)}, s32[1,128]{1,0:T(1,128)S(1)}, u32[]{:S(2)}, u32[]{:S(2)}) collective-permute-start(s32[1,128]{1,0:T(1,128)S(1)} %get-tuple-element.55), channel_id=1, source_target_pairs={{0,14},{1,15},{2,12},{3,13},{4,10},{5,11},{6,8},{7,9},{8,6},{9,7},... | collective-permute-start | bytes 1544 | tf_op jit(solution)/shard_map/ppermute | solution.py:157
  58.0 5.7 %collective-permute-start.14 = (s32[1,128]{1,0:T(1,128)S(1)}, s32[1,128]{1,0:T(1,128)S(1)}, u32[]{:S(2)}, u32[]{:S(2)}) collective-permute-start(s32[1,128]{1,0:T(1,128)S(1)} %get-tuple-element.54), channel_id=1, source_target_pairs={{0,15},{1,14},{2,13},{3,12},{4,11},{5,10},{6,9},{7,8},{8,7},{9,6},... | collective-permute-start | bytes 1544 | tf_op jit(solution)/shard_map/ppermute | solution.py:157
  58.0 5.7 %collective-permute-start.1 = (s32[1,128]{1,0:T(1,128)S(1)}, s32[1,128]{1,0:T(1,128)S(1)}, u32[]{:S(2)}, u32[]{:S(2)}) collective-permute-start(s32[1,128]{1,0:T(1,128)S(1)} %get-tuple-element.67), channel_id=1, source_target_pairs={{0,2},{1,3},{2,0},{3,1},{4,6},{5,7},{6,4},{7,5},{8,10},{9,11},{10,... | collective-permute-start | bytes 1544 | tf_op jit(solution)/shard_map/ppermute | solution.py:157
  59.2 4.4 %collective-permute-start.2 = (s32[1,128]{1,0:T(1,128)S(1)}, s32[1,128]{1,0:T(1,128)S(1)}, u32[]{:S(2)}, u32[]{:S(2)}) collective-permute-start(s32[1,128]{1,0:T(1,128)S(1)} %get-tuple-element.66), channel_id=1, source_target_pairs={{0,3},{1,2},{2,1},{3,0},{4,7},{5,6},{6,5},{7,4},{8,11},{9,10},{10,... | collective-permute-start | bytes 1544 | tf_op jit(solution)/shard_map/ppermute | solution.py:157
  133.5 3.6 %copy-start.2 = (f32[4,2,256,144]{2,3,1,0:T(8,128)S(1)}, f32[4,2,256,144]{2,3,1,0:T(8,128)}, u32[]{:S(2)}) copy-start(f32[4,2,256,144]{2,3,1,0:T(8,128)} %all-reduce.2.cloned.1.call-done) | copy-start | bytes 3538948
  139.6 7.0 %slice-start = ((s8[6291456]{0:T(1024)(128)(4,1)}), s8[4194304]{0:T(1024)(128)(4,1)S(1)}, s32[]{:S(2)}) async-start(s8[6291456]{0:T(1024)(128)(4,1)} %bitcast.287), calls=%async_computation.2 | async-start | bytes 8388608
  141.8 4.8 %slice-start.1 = ((s8[6291456]{0:T(1024)(128)(4,1)}), s8[2097152]{0:T(1024)(128)(4,1)S(1)}, s32[]{:S(2)}) async-start(s8[6291456]{0:T(1024)(128)(4,1)} %bitcast.287), calls=%async_computation.3 | async-start | bytes 4194304
  196.7 2.8 %copy-start.1 = (f32[128,2,256]{2,1,0:T(2,128)S(1)}, f32[128,2,256]{2,1,0:T(2,128)}, u32[]{:S(2)}) copy-start(f32[128,2,256]{2,1,0:T(2,128)} %param.9) | copy-start | bytes 786436
Sparse Core Ops, SparseCore 0:
  36.5 96.9 all-reduce.1
